TPU v7x, 128 devices: a whole 4x4x4 slice. The times are simulated.
128 devices in a mesh: grp: 8 (over x, core), dev: 16 (over y, z).
Axes of the slice: x: 4, y: 4, z: 4, core: 2. Of those that a mesh axis runs over, the one named last changes fastest.
Arguments:
- sep_inv: bfloat16 [4096, 4096], P('grp', 'dev'), may hold values from -0.125 to 0.125
- panels: bfloat16 [8, 96, 2048, 128], P('grp', 'dev'), may hold values from -1.1953125 to 1.1953125
- diag_inverse: bfloat16 [8, 96, 768, 128], P('grp', 'dev'), may hold values from -6 to 6
- widths: int32 [8, 32], P('grp'), may hold values from 1 to 6, 96 in all within a row
- ancestors: int32 [8, 32, 16], P('grp'), may hold values from 0 to 31, as said below
Outputs:
- off_diag: bfloat16 [8, 96, 2048, 128], P('grp', 'dev')
- diag_panels: bfloat16 [8, 96, 768, 128], P('grp', 'dev')
Inputs may be any that keep to these rules, and one draw needn't show every extreme that they name: `widths`: each row of a subtree sums to 96. `ancestors`: each supernode's list holds 16 different separator tile numbers in increasing order.
All inputs are finite; a program needn't handle non-finite values.
Results may differ from a plain program's by a relative error of at most 0.0046.
Values may be sent and summed in bfloat16 or wider, within the bound.
A program may use at most 320 MiB of HBM per device.

v0:
```python
import jax
import jax.numpy as jnp
from jax import lax
from jax.sharding import PartitionSpec as P


def extended_2(cells, sides, width):
    for axis, dim in sides:
        count = lax.axis_size(axis)
        ends = count - 1
        head = lax.slice_in_dim(cells, 0, width, axis=dim)
        tail = lax.slice_in_dim(cells, cells.shape[dim] - width, cells.shape[dim], axis=dim)
        cells = jnp.concatenate(
            [
                lax.ppermute(tail, axis, [(i, (i + 1) % count) for i in range(ends)]),
                cells,
                lax.ppermute(head, axis, [((i + 1) % count, i) for i in range(ends)]),
            ],
            axis=dim,
        )
    return cells


def on_device(sep_inv, panels, diag_inverse, widths, ancestors):
    group_count = lax.axis_size("grp")
    device_count = lax.axis_size("dev")
    rows_local = sep_inv.shape[0]
    cols_local = sep_inv.shape[1]
    stacked = lax.all_gather(sep_inv[None], ("grp", "dev"), axis=0, tiled=True)
    whole_sep = stacked.reshape(group_count, device_count, rows_local, cols_local)
    whole_sep = whole_sep.transpose(0, 2, 1, 3).reshape(
        group_count * rows_local, device_count * cols_local
    )
    block = panels.shape[3]
    anc_rows = panels.shape[2]
    anc_tiles = anc_rows // block
    local_units = panels.shape[1]
    max_tiles = diag_inverse.shape[2] // block
    sep_order = whole_sep.shape[0]
    count_blocks = sep_order // block
    row_tiles = whole_sep.reshape(count_blocks, block, sep_order)
    extended = extended_2(panels, (("dev", 1),), max_tiles - 1)
    width_row = widths[0]
    anc_table = ancestors[0]
    supernodes = width_row.shape[0]
    ends = jnp.cumsum(width_row)
    starts = ends - width_row
    position = lax.axis_index("dev") * local_units + jnp.arange(local_units, dtype=jnp.int32)
    owner = jnp.sum((ends[None, :] <= position[:, None]).astype(jnp.int32), axis=1)
    one_hot = (jnp.arange(supernodes, dtype=jnp.int32)[None, :] == owner[:, None]).astype(jnp.int32)
    column = position - jnp.sum(one_hot * starts[None, :], axis=1)
    width_unit = jnp.sum(one_hot * width_row[None, :], axis=1)
    blocks = jnp.sum(one_hot[:, :, None] * anc_table[None, :, :], axis=1)
    tile_ids = jnp.arange(count_blocks, dtype=jnp.int32)

    def per_unit(unit_idx):
        chosen = blocks[unit_idx]
        rows_pick = jnp.take(row_tiles, chosen, axis=0).reshape(anc_rows, sep_order)
        placing = (tile_ids[:, None] == chosen[None, :]).astype(jnp.bfloat16)
        panel_flat = panels[0, unit_idx].reshape(anc_tiles, block * block)
        spread = jnp.dot(placing, panel_flat, preferred_element_type=jnp.float32)
        spread = spread.astype(jnp.bfloat16).reshape(sep_order, block)
        product = jnp.dot(rows_pick, spread, preferred_element_type=jnp.float32)
        result_x = (-product).astype(jnp.bfloat16)
        start_at = unit_idx + max_tiles - 1 - column[unit_idx]
        related = lax.dynamic_slice_in_dim(extended[0], start_at, max_tiles, 0)
        inner = jnp.einsum("jrb,rc->jbc", related, result_x, preferred_element_type=jnp.float32)
        keep = (jnp.arange(max_tiles, dtype=jnp.int32) < width_unit[unit_idx]).astype(jnp.float32)
        diag_block = (
            diag_inverse[0, unit_idx].astype(jnp.float32).reshape(max_tiles, block, block) - inner
        ) * keep[:, None, None]
        return (result_x, diag_block.reshape(max_tiles * block, block).astype(jnp.bfloat16))

    off_diag, diag_panels = lax.map(per_unit, jnp.arange(local_units, dtype=jnp.int32))
    return (off_diag[None], diag_panels[None])


def solution(mesh):
    placed = (
        P("grp", "dev"),
        P("grp", "dev", None, None),
        P("grp", "dev", None, None),
        P("grp", None),
        P("grp", None, None),
    )
    return jax.shard_map(
        on_device,
        mesh=mesh,
        in_specs=placed,
        out_specs=(P("grp", "dev", None, None), P("grp", "dev", None, None)),
        check_vma=False,
    )
```

profile of v0, /device:TPU:1, one launch (start us, length us, event | category | flops | bytes accessed | tf_op | source)
XLA Modules:
  0.0 488.8 jit_solution(15844366094010139155)
XLA Ops:
  14.1 5.9 %collective-permute-start = (bf16[1,5,2048,128]{2,3,1,0:T(8,128)(2,1)}, bf16[1,5,2048,128]{2,3,1,0:T(8,128)(2,1)}, u32[]{:S(2)}, u32[]{:S(2)}) collective-permute-start(bf16[1,5,2048,128]{2,3,1,0:T(8,128)(2,1)} %get-tuple-element.293), channel_id=1, source_target_pairs={{0,1},{1,2},{2,3},{3,4},{4,5},{5,6},{6,7},{7,8},{8,9},{9,10},{10,1... | collective-permute-start | bytes 7864328 | tf_op jit(solution)/shard_map/ppermute | solution.py:15
  22.2 54.9 %collective-permute-done = bf16[1,5,2048,128]{2,3,1,0:T(8,128)(2,1)} collective-permute-done((bf16[1,5,2048,128]{2,3,1,0:T(8,128)(2,1)}, bf16[1,5,2048,128]{2,3,1,0:T(8,128)(2,1)}, u32[]{:S(2)}, u32[]{:S(2)}) %collective-permute-start) | collective-permute-done | bytes 2621472 | tf_op jit(solution)/shard_map/ppermute | solution.py:15
  82.5 6.3 %pad_maximum_fusion = bf16[1,16,2048,128]{2,3,1,0:T(8,128)(2,1)} fusion(bf16[1,5,2048,128]{2,3,1,0:T(8,128)(2,1)} %collective-permute-done.1, bf16[1,6,2048,128]{2,3,1,0:T(8,128)(2,1)S(1)} %copy.21, bf16[1,5,2048,128]{2,3,1,0:T(8,128)(2,1)} %collective-permute-done), kind=kLoop, calls=%fused_computation.29 | loop fusion | flops 8388608 | bytes 16777216 | tf_op jit(solution)/shard_map/concatenate | solution.py:13
  88.8 80.5 %all-gather.3.cloned.1.call-done = bf16[65536,256]{1,0:T(8,128)(2,1)} async-done(((bf16[512,256]{1,0:T(8,128)(2,1)}), bf16[65536,256]{1,0:T(8,128)(2,1)}) %all-gather.3.cloned.1.call-update) | async-done | bytes 33554448 | tf_op jit(solution)/shard_map/all_gather | solution.py:29
  169.3 31.2 %copy.25 = bf16[8,16,512,256]{3,1,2,0:T(8,128)(2,1)} copy(bf16[8,16,512,256]{3,2,1,0:T(8,128)(2,1)} %bitcast.82) | data formatting | bytes 67108864 | tf_op jit(solution)/shard_map/reshape | solution.py:30
  200.5 49.9 %reshape_reshape.3 = bf16[32,128,4096]{2,1,0:T(8,128)(2,1)} reshape(bf16[8,512,16,256]{3,2,1,0:T(8,128)(2,1)} %bitcast.81) | data formatting | bytes 67108864 | tf_op jit(solution)/shard_map/reshape;reshape | solution.py:41
  250.4 231.6 %while.17 = (s32[]{:T(128)}, bf16[6,2048,128]{2,1,0:T(8,128)(2,1)}, bf16[6,768,128]{2,1,0:T(8,128)(2,1)}, s32[6]{0:T(128)S(1)}, s32[6,16]{1,0:T(8,128)S(1)}, /*i...) while((s32[]{:T(128)}, bf16[6,2048,128]{2,1,0:T(8,128)(2,1)}, ...), condition=%wide.region_6.7_spmd.clone, body=%wide.region_5.6_spmd.clone.sunk | while | flops 2576746240 | bytes 96605016 | solution.py:74
  259.7 11.8 %gather_fusion = bf16[16,128,4096]{2,1,0:T(8,128)(2,1)} fusion(bf16[32,128,4096]{2,1,0:T(8,128)(2,1)} %get-tuple-element.407, s32[1024]{0:T(1024)S(1)} %pad_clamp_fusion.2), kind=kCustom, calls=%fused_computation.clone.clone.1 | custom fusion | bytes 33554496 | tf_op jit(solution)/shard_map/while/body/eval_jaxpr/jit(_take)/gather | solution.py:58
  271.4 8.5 %broadcast_select_fusion.2 = bf16[16,128,4096]{2,1,0:T(8,128)(2,1)S(1)} fusion(bf16[16,128,4096]{2,1,0:T(8,128)(2,1)} %gather_fusion, pred[16]{0:T(512)(128)(4,1)S(1)} %get-tuple-element.366), kind=kLoop, calls=%fused_computation.3.clone.1 | loop fusion | flops 8388608 | bytes 33554448 | tf_op jit(solution)/shard_map/while/body/eval_jaxpr/jit(_take)/select_n | solution.py:58
  280.0 5.5 %bitcast_dynamic-update-slice_fusion.4 = (bf16[6,2048,128]{2,1,0:T(8,128)(2,1)}, bf16[2048,128]{1,0:T(8,128)(2,1)S(1)}) fusion(bf16[6,2048,128]{2,1,0:T(8,128)(2,1)} %get-tuple-element.387, s32[]{:T(128)S(6)} %copy.31, bf16[2048,4096]{1,0:T(8,128)(2,1)S(1)} %bitcast.80, bf16[4096,128]{1,0:T(8,128)(2,1)S(1)} %reshape.215), kind=kOutput, calls=%fused_computation.13.clone.1 | convolution fusion | flops 2148007936 | bytes 18874372 | tf_op jit(solution)/shard_map/while/body/eval_jaxpr/dot_general | solution.py:63
  298.3 11.8 %gather_fusion = bf16[16,128,4096]{2,1,0:T(8,128)(2,1)} fusion(bf16[32,128,4096]{2,1,0:T(8,128)(2,1)} %get-tuple-element.407, s32[1024]{0:T(1024)S(1)} %pad_clamp_fusion.2), kind=kCustom, calls=%fused_computation.clone.clone.1 | custom fusion | bytes 33554496 | tf_op jit(solution)/shard_map/while/body/eval_jaxpr/jit(_take)/gather | solution.py:58
  310.0 8.5 %broadcast_select_fusion.2 = bf16[16,128,4096]{2,1,0:T(8,128)(2,1)S(1)} fusion(bf16[16,128,4096]{2,1,0:T(8,128)(2,1)} %gather_fusion, pred[16]{0:T(512)(128)(4,1)S(1)} %get-tuple-element.366), kind=kLoop, calls=%fused_computation.3.clone.1 | loop fusion | flops 8388608 | bytes 33554448 | tf_op jit(solution)/shard_map/while/body/eval_jaxpr/jit(_take)/select_n | solution.py:58
  318.5 5.5 %bitcast_dynamic-update-slice_fusion.4 = (bf16[6,2048,128]{2,1,0:T(8,128)(2,1)}, bf16[2048,128]{1,0:T(8,128)(2,1)S(1)}) fusion(bf16[6,2048,128]{2,1,0:T(8,128)(2,1)} %get-tuple-element.387, s32[]{:T(128)S(6)} %copy.31, bf16[2048,4096]{1,0:T(8,128)(2,1)S(1)} %bitcast.80, bf16[4096,128]{1,0:T(8,128)(2,1)S(1)} %reshape.215), kind=kOutput, calls=%fused_computation.13.clone.1 | convolution fusion | flops 2148007936 | bytes 18874372 | tf_op jit(solution)/shard_map/while/body/eval_jaxpr/dot_general | solution.py:63
  336.8 11.8 %gather_fusion = bf16[16,128,4096]{2,1,0:T(8,128)(2,1)} fusion(bf16[32,128,4096]{2,1,0:T(8,128)(2,1)} %get-tuple-element.407, s32[1024]{0:T(1024)S(1)} %pad_clamp_fusion.2), kind=kCustom, calls=%fused_computation.clone.clone.1 | custom fusion | bytes 33554496 | tf_op jit(solution)/shard_map/while/body/eval_jaxpr/jit(_take)/gather | solution.py:58
  348.6 8.5 %broadcast_select_fusion.2 = bf16[16,128,4096]{2,1,0:T(8,128)(2,1)S(1)} fusion(bf16[16,128,4096]{2,1,0:T(8,128)(2,1)} %gather_fusion, pred[16]{0:T(512)(128)(4,1)S(1)} %get-tuple-element.366), kind=kLoop, calls=%fused_computation.3.clone.1 | loop fusion | flops 8388608 | bytes 33554448 | tf_op jit(solution)/shard_map/while/body/eval_jaxpr/jit(_take)/select_n | solution.py:58
  357.1 5.5 %bitcast_dynamic-update-slice_fusion.4 = (bf16[6,2048,128]{2,1,0:T(8,128)(2,1)}, bf16[2048,128]{1,0:T(8,128)(2,1)S(1)}) fusion(bf16[6,2048,128]{2,1,0:T(8,128)(2,1)} %get-tuple-element.387, s32[]{:T(128)S(6)} %copy.31, bf16[2048,4096]{1,0:T(8,128)(2,1)S(1)} %bitcast.80, bf16[4096,128]{1,0:T(8,128)(2,1)S(1)} %reshape.215), kind=kOutput, calls=%fused_computation.13.clone.1 | convolution fusion | flops 2148007936 | bytes 18874372 | tf_op jit(solution)/shard_map/while/body/eval_jaxpr/dot_general | solution.py:63
  375.4 11.8 %gather_fusion = bf16[16,128,4096]{2,1,0:T(8,128)(2,1)} fusion(bf16[32,128,4096]{2,1,0:T(8,128)(2,1)} %get-tuple-element.407, s32[1024]{0:T(1024)S(1)} %pad_clamp_fusion.2), kind=kCustom, calls=%fused_computation.clone.clone.1 | custom fusion | bytes 33554496 | tf_op jit(solution)/shard_map/while/body/eval_jaxpr/jit(_take)/gather | solution.py:58
  387.2 8.5 %broadcast_select_fusion.2 = bf16[16,128,4096]{2,1,0:T(8,128)(2,1)S(1)} fusion(bf16[16,128,4096]{2,1,0:T(8,128)(2,1)} %gather_fusion, pred[16]{0:T(512)(128)(4,1)S(1)} %get-tuple-element.366), kind=kLoop, calls=%fused_computation.3.clone.1 | loop fusion | flops 8388608 | bytes 33554448 | tf_op jit(solution)/shard_map/while/body/eval_jaxpr/jit(_take)/select_n | solution.py:58
  395.8 5.5 %bitcast_dynamic-update-slice_fusion.4 = (bf16[6,2048,128]{2,1,0:T(8,128)(2,1)}, bf16[2048,128]{1,0:T(8,128)(2,1)S(1)}) fusion(bf16[6,2048,128]{2,1,0:T(8,128)(2,1)} %get-tuple-element.387, s32[]{:T(128)S(6)} %copy.31, bf16[2048,4096]{1,0:T(8,128)(2,1)S(1)} %bitcast.80, bf16[4096,128]{1,0:T(8,128)(2,1)S(1)} %reshape.215), kind=kOutput, calls=%fused_computation.13.clone.1 | convolution fusion | flops 2148007936 | bytes 18874372 | tf_op jit(solution)/shard_map/while/body/eval_jaxpr/dot_general | solution.py:63
  414.1 11.8 %gather_fusion = bf16[16,128,4096]{2,1,0:T(8,128)(2,1)} fusion(bf16[32,128,4096]{2,1,0:T(8,128)(2,1)} %get-tuple-element.407, s32[1024]{0:T(1024)S(1)} %pad_clamp_fusion.2), kind=kCustom, calls=%fused_computation.clone.clone.1 | custom fusion | bytes 33554496 | tf_op jit(solution)/shard_map/while/body/eval_jaxpr/jit(_take)/gather | solution.py:58
  425.8 8.5 %broadcast_select_fusion.2 = bf16[16,128,4096]{2,1,0:T(8,128)(2,1)S(1)} fusion(bf16[16,128,4096]{2,1,0:T(8,128)(2,1)} %gather_fusion, pred[16]{0:T(512)(128)(4,1)S(1)} %get-tuple-element.366), kind=kLoop, calls=%fused_computation.3.clone.1 | loop fusion | flops 8388608 | bytes 33554448 | tf_op jit(solution)/shard_map/while/body/eval_jaxpr/jit(_take)/select_n | solution.py:58
  434.3 5.5 %bitcast_dynamic-update-slice_fusion.4 = (bf16[6,2048,128]{2,1,0:T(8,128)(2,1)}, bf16[2048,128]{1,0:T(8,128)(2,1)S(1)}) fusion(bf16[6,2048,128]{2,1,0:T(8,128)(2,1)} %get-tuple-element.387, s32[]{:T(128)S(6)} %copy.31, bf16[2048,4096]{1,0:T(8,128)(2,1)S(1)} %bitcast.80, bf16[4096,128]{1,0:T(8,128)(2,1)S(1)} %reshape.215), kind=kOutput, calls=%fused_computation.13.clone.1 | convolution fusion | flops 2148007936 | bytes 18874372 | tf_op jit(solution)/shard_map/while/body/eval_jaxpr/dot_general | solution.py:63
  452.6 11.8 %gather_fusion = bf16[16,128,4096]{2,1,0:T(8,128)(2,1)} fusion(bf16[32,128,4096]{2,1,0:T(8,128)(2,1)} %get-tuple-element.407, s32[1024]{0:T(1024)S(1)} %pad_clamp_fusion.2), kind=kCustom, calls=%fused_computation.clone.clone.1 | custom fusion | bytes 33554496 | tf_op jit(solution)/shard_map/while/body/eval_jaxpr/jit(_take)/gather | solution.py:58
  464.4 8.5 %broadcast_select_fusion.2 = bf16[16,128,4096]{2,1,0:T(8,128)(2,1)S(1)} fusion(bf16[16,128,4096]{2,1,0:T(8,128)(2,1)} %gather_fusion, pred[16]{0:T(512)(128)(4,1)S(1)} %get-tuple-element.366), kind=kLoop, calls=%fused_computation.3.clone.1 | loop fusion | flops 8388608 | bytes 33554448 | tf_op jit(solution)/shard_map/while/body/eval_jaxpr/jit(_take)/select_n | solution.py:58
  (108 shorter events, 76.3 us)
Async XLA Ops:
  7.2 162.2 %all-gather.3.cloned.1.call-start = ((), (), s32[]{:S(2)}) async-start(), calls=%async_computation | async-start | bytes 33816576 | tf_op jit(solution)/shard_map/all_gather | solution.py:29
  11.1 10.2 %copy-start.1 = (s32[1,32]{1,0:T(1,128)S(1)}, s32[1,32]{1,0:T(1,128)}, u32[]{:S(2)}) copy-start(s32[1,32]{1,0:T(1,128)} %param.10) | copy-start | bytes 388
  11.1 10.7 %copy-start = (s32[1,32,16]{1,2,0:T(8,128)S(1)}, s32[1,32,16]{1,2,0:T(8,128)}, u32[]{:S(2)}) copy-start(s32[1,32,16]{1,2,0:T(8,128)} %param.11) | copy-start | bytes 6148
  14.1 63.0 %collective-permute-start = (bf16[1,5,2048,128]{2,3,1,0:T(8,128)(2,1)}, bf16[1,5,2048,128]{2,3,1,0:T(8,128)(2,1)}, u32[]{:S(2)}, u32[]{:S(2)}) collective-permute-start(bf16[1,5,2048,128]{2,3,1,0:T(8,128)(2,1)} %get-tuple-element.293), channel_id=1, source_target_pairs={{0,1},{1,2},{2,3},{3,4},{4,5},{5,6},{6,7},{7,8},{8,9},{9,10},{10,1... | collective-permute-start | bytes 7864328 | tf_op jit(solution)/shard_map/ppermute | solution.py:15
  20.0 62.5 %collective-permute-start.1 = (bf16[1,5,2048,128]{2,3,1,0:T(8,128)(2,1)}, bf16[1,5,2048,128]{2,3,1,0:T(8,128)(2,1)}, u32[]{:S(2)}, u32[]{:S(2)}) collective-permute-start(bf16[1,5,2048,128]{2,3,1,0:T(8,128)(2,1)} %get-tuple-element.294), channel_id=1, source_target_pairs={{1,0},{2,1},{3,2},{4,3},{5,4},{6,5},{7,6},{8,7},{9,8},{10,9},{11,1... | collective-permute-start | bytes 7864328 | tf_op jit(solution)/shard_map/ppermute | solution.py:17
Sparse Core Ops, SparseCore 0:
  11.1 158.1 all-gather.2
where the time goes:
time: 492 us; the launch traced here: 489 us
  local copies, waits for them, and re-layouts  191 us (39%)
  waiting for transfers between devices  141 us (29%)
  other arithmetic  62.4 us (13%)
  matrix products  52.4 us (11%)
  loops' own time  20.7 us (4%)
  between operations  14.1 us (3%)
  starting transfers between devices  7.21 us (1%)
    all_gather x1, waiting for transfers between devices, on_device(): stacked = lax.all_gather(sep_inv[None], ('grp', 'dev'), axis=0, tiled=True)  80.5 us
    gather x6, local copies, waits for them, and re-layouts, per_unit(): rows_pick = jnp.take(row_tiles, chosen, axis=0).reshape(anc_rows, sep_order)  70.6 us
    ppermute x1, waiting for transfers between devices, extended_2(): lax.ppermute(tail, axis, [(i, (i + 1) % count) for i in range(ends)])  54.9 us
    select_n x12, other arithmetic, per_unit(): rows_pick = jnp.take(row_tiles, chosen, axis=0).reshape(anc_rows, sep_order)  51.1 us
    another operation x1, local copies, waits for them, and re-layouts, on_device(): row_tiles = whole_sep.reshape(count_blocks, block, sep_order)  49.9 us
    dot_general x6, matrix products, per_unit(): product = jnp.dot(rows_pick, spread, preferred_element_type=jnp.float32)  32.8 us
    reshape x1, local copies, waits for them, and re-layouts, on_device(): stacked.reshape(group_count, device_count, rows_local, cols_local)  31.2 us
    another operation x1, loops' own time, on_device(): lax.map(per_unit, jnp.arange(local_units, dtype=jnp.int32))  20.7 us
  transfers between devices with their start and end apart: 3, of which 3 were waited for; matrix products, arithmetic and copies ran while one was open for 3% of the time, Pallas kernels for 0%

commit v1 on v0

v1 whole, which is shorter than its diff:
```python
import functools
import heapq

import jax
import jax.numpy as jnp
from jax import lax
from jax.experimental import pallas as pl
from jax.experimental.pallas import tpu as pltpu
from jax.sharding import PartitionSpec as P

MESH = pl.DeviceIdType.MESH
F32 = jnp.float32
BF16 = jnp.bfloat16
ORDER = (("y", "z", "x"), ("z", "y", "x"), ("z", "x", "y"), ("y", "x", "z"))
B = 128
LOCAL = 6
EDGE = 5
ANC = 16
TILES = 32
NSG = 32
CHUNKS = 16
KC = 256
SPREADS = 4
HALOS = 20


def plan():
    rate, latency, piece, edge = 44e3, 2.2, B * KC * 2, 512 * B * 2
    steps, free, heap, got, tasks = [], {}, [], {}, []
    clock = 0.0
    cost = {"A": 1.4, "B": 2.1, "C": 2.1}

    def send(m):
        part, phase, _, s, kind = m
        link = (ORDER[part][phase - 1], s)
        size = piece * (4 if phase == 3 else 1) // (2 if kind == "half" else 1)
        free[link] = max(clock, free.get(link, 0.0)) + size / rate
        heapq.heappush(heap, (free[link] + latency, len(steps), m))
        steps.append(("send", m))

    def near(part, phase, a):
        for s in (1, -1):
            send((part, phase, a, s, "near"))

    def count(key):
        got[key] = got.get(key, 0) + 1
        return got[key]

    def plane(part, rel):
        if part < 2:
            if count(("A", rel)) == 8:
                tasks.extend(("A", rel, i) for i in range(3))
        elif count((part, "plane", rel)) == 4:
            tasks.append(("B" if part == 2 else "C", rel, count((part, "order"))))

    def handle(m):
        part, phase, a, s, kind = m
        if phase == 1:
            if kind == "near":
                send((part, 1, 0, s, "half"))
                near(part, 2, -s)
                full = count((part, 1))
            elif count((part, 1, "far")) == 2:
                near(part, 2, 2)
                full = count((part, 1))
            else:
                full = 0
            if full == 3:
                near(part, 3, 0)
                plane(part, 0)
        elif phase == 2:
            if kind == "near":
                send((part, 2, a, s, "half"))
                if count((part, 2, -s)) == 4:
                    near(part, 3, -s)
                    plane(part, 0)
            elif count((part, 2, 2)) == 8:
                near(part, 3, 2)
                plane(part, 0)
        elif kind == "near":
            send((part, 3, a, s, "half"))
            plane(part, -s)
        elif count((part, 3, a, "far")) == 2:
            plane(part, 2)

    for phase in (1, 2):
        for part in range(4):
            near(part, phase, 0)
    edges = 0
    while heap or tasks:
        while heap and heap[0][0] <= clock:
            m = heapq.heappop(heap)[2]
            steps.append(("wait", m))
            handle(m)
        while edges < HALOS and 8 < clock and free[("z", 1)] < clock + 4:
            for s in (1, -1):
                free[("z", s)] = max(clock, free[("z", s)]) + edge / rate
            steps.append(("edge", edges))
            edges += 1
        if tasks:
            task = tasks.pop(0)
            steps.append(("task",) + task)
            clock += cost[task[0]]
        elif heap:
            clock = max(clock, heap[0][0])
    return steps + [("edge", i) for i in range(edges, HALOS)]


def spans(widths, position):
    def step(k, carry):
        end, owner, start, width = carry
        w = widths[0, k]
        inside = [(position + u >= end) & (position + u < end + w) for u in range(LOCAL)]
        owner = tuple(jnp.where(i, k, o) for i, o in zip(inside, owner))
        start = tuple(jnp.where(i, end, o) for i, o in zip(inside, start))
        width = tuple(jnp.where(i, w, o) for i, o in zip(inside, width))
        return end + w, owner, start, width

    zeros = (jnp.int32(0),) * LOCAL
    _, owner, start, width = lax.fori_loop(0, NSG, step, (jnp.int32(0), zeros, zeros, zeros))
    return owner, start, width


def spread_kernel(widths, ancestors, panel, out, table, spot):
    u = pl.program_id(0)

    @pl.when(u == 0)
    def _():
        owner, start, width = spans(widths, lax.axis_index("dev") * LOCAL)
        for v in range(LOCAL):
            table[0, v] = owner[v]
            table[1, v] = lax.axis_index("dev") * LOCAL + v - start[v]
            table[2, v] = width[v]
            for t in range(TILES):
                spot[v, t] = ANC
        for v in range(LOCAL):
            for a in range(ANC):
                spot[v, ancestors[0, owner[v], a]] = a

    for t in range(TILES):
        a = spot[u, t]
        rows = pl.ds(pl.multiple_of(jnp.minimum(a, ANC - 1) * B, B), B)
        value = panel[0, 0, rows, :]
        out[t // 2, (t % 2) * B:(t % 2 + 1) * B, :] = jnp.where(a < ANC, value, jnp.zeros_like(value))


def gather_kernel(
    steps, sep, panels, spread, y_out, left_out, right_out,
    blocks, own, other, total, stage_own, stage_other,
    load_sem, own_sem, send_sem, recv_sem, half_send, half_recv, y_local, y_send, y_recv, edge_send, edge_recv,
):
    grp, dev = lax.axis_index("grp"), lax.axis_index("dev")
    core = lax.rem(grp, 2)
    at = {"x": grp // 2, "y": dev // 4, "z": lax.rem(dev, 4)}

    def moved(axis, by):
        return lax.rem(at[axis] + by + 4, 4)

    def device(axis, by):
        to = dict(at)
        to[axis] = moved(axis, by)
        return (to["x"] * 2 + core, to["y"] * 4 + to["z"])

    partner = (at["x"] * 2 + 1 - core, dev)
    ahead, behind = (grp, lax.rem(dev + 1, 16)), (grp, lax.rem(dev + 15, 16))

    loads = [
        pltpu.make_async_copy(
            sep.at[pl.ds(p * B, B)], blocks.at[p, at["x"], at["y"], at["z"]], load_sem.at[p]
        )
        for p in range(4)
    ]
    own_load = pltpu.make_async_copy(spread, own, own_sem)
    for c in loads:
        c.start()
    own_load.start()
    barrier = pltpu.get_barrier_semaphore()
    greeted = [device(a, s) for a in ("x", "y", "z") for s in (1, -1)] + [partner, ahead, behind]
    for d in greeted:
        pl.semaphore_signal(barrier, inc=1, device_id=d, device_id_type=MESH)
    for c in loads:
        c.wait()
    pl.semaphore_wait(barrier, len(greeted))

    number = {m: i for i, m in enumerate(s[1] for s in steps if s[0] == "send")}

    def message(m, arriving):
        part, phase, a, s, kind = m
        axes = ORDER[part]
        axis = axes[phase - 1]
        where = dict(at)
        if phase == 2:
            where[axes[0]] = moved(axes[0], a)
        if phase == 3:
            where[axes[0]] = slice(None)
            where[axes[1]] = moved(axes[1], a)
        gone = (0 if kind == "near" else 1) + (1 if arriving else 0)
        where[axis] = moved(axis, -s * gone)
        columns = slice(None) if kind == "near" else pl.ds(0 if s == 1 else B, B)
        ref = blocks.at[part, where["x"], where["y"], where["z"], slice(None), columns]
        if phase == 3:
            ref = blocks.at[part, where["x"], where["y"], where["z"], :, columns]
        return pltpu.make_async_remote_copy(
            src_ref=ref, dst_ref=ref, send_sem=send_sem.at[number[m]], recv_sem=recv_sem.at[number[m]],
            device_id=device(axis, s), device_id_type=MESH,
        )

    def spread_copy(i):
        some = pl.ds(CHUNKS // SPREADS * i, CHUNKS // SPREADS)
        return pltpu.make_async_remote_copy(
            src_ref=spread.at[some], dst_ref=other.at[some], send_sem=half_send.at[i], recv_sem=half_recv.at[i],
            device_id=partner, device_id_type=MESH,
        )

    def edge_copy(i):
        t, rows = i // 4, pl.ds((i % 4) * 512, 512)
        return [
            pltpu.make_async_remote_copy(
                src_ref=panels.at[0, LOCAL - EDGE + t, rows], dst_ref=left_out.at[t, rows],
                send_sem=edge_send.at[0], recv_sem=edge_recv.at[0], device_id=ahead, device_id_type=MESH,
            ),
            pltpu.make_async_remote_copy(
                src_ref=panels.at[0, t, rows], dst_ref=right_out.at[t, rows],
                send_sem=edge_send.at[1], recv_sem=edge_recv.at[1], device_id=behind, device_id_type=MESH,
            ),
        ]

    def results(i, x, tiles):
        here, there = pl.ds(tiles, 2 if tiles == 0 else 1), 2 * x + core
        return (
            pltpu.make_async_copy(stage_own.at[:, x, here], y_out.at[:, there, here], y_local.at[i]),
            pltpu.make_async_remote_copy(
                src_ref=stage_other.at[:, x, here], dst_ref=y_out.at[:, there, here],
                send_sem=y_send.at[i], recv_sem=y_recv.at[i], device_id=partner, device_id_type=MESH,
            ),
        )

    def arrived(i, x, tiles):
        here, there = pl.ds(tiles, 2 if tiles == 0 else 1), 2 * x + 1 - core
        return pltpu.make_async_remote_copy(
            src_ref=y_out.at[:, there, here], dst_ref=y_out.at[:, there, here],
            send_sem=y_send.at[i], recv_sem=y_recv.at[i], device_id=partner, device_id_type=MESH,
        )

    queued = []

    def put(x, tiles):
        i = len(queued)
        queued.append((i, x, tiles))
        for c in results(i, x, tiles):
            c.start()

    def task_a(rel, n):
        x = moved("x", rel)
        cols = pl.ds(n * 256, 256)
        for source, stage in ((own, stage_own), (other, stage_other)):
            acc = jnp.zeros((2 * B, 256), F32)
            for k in range(CHUNKS):
                lhs = blocks[0:2, x, k // 4, k % 4].reshape(2 * B, KC)
                acc = acc + jnp.dot(lhs, source[k, :, cols], preferred_element_type=F32)
            value = acc.astype(BF16)
            for p in range(2):
                for v in range(2):
                    stage[2 * n + v, x, p] = value[p * B:(p + 1) * B, v * B:(v + 1) * B]

    def task_bc(part, rel, nth):
        axis = "y" if part == 2 else "z"
        fixed = moved(axis, rel)
        for h, (source, stage) in enumerate(((own, stage_own), (other, stage_other))):
            def column(n, carry):
                acc = jnp.zeros((4 * B, 256), F32)
                cols = pl.ds(pl.multiple_of(n * 256, 256), 256)
                for k in range(4):
                    yy, zz = (fixed, k) if part == 2 else (k, fixed)
                    lhs = blocks[part, :, yy, zz].reshape(4 * B, KC)
                    acc = acc + jnp.dot(lhs, source[yy * 4 + zz, :, cols], preferred_element_type=F32)
                slot = (part - 2, 3 * h + n)
                if nth == 1:
                    total[slot] = acc
                elif nth < 4:
                    total[slot] = total[slot] + acc
                else:
                    value = (total[slot] + acc).astype(BF16)
                    for x in range(4):
                        for v in range(2):
                            stage[2 * n + v, x, part] = value[x * B:(x + 1) * B, v * B:(v + 1) * B]
                return carry

            lax.fori_loop(0, 3, column, 0)

    for j in range(SPREADS):
        spread_copy(j).start()
    got_other = False
    for step in steps:
        if step[0] == "send":
            message(step[1], False).start()
        elif step[0] == "wait":
            message(step[1], True).wait_recv()
        elif step[0] == "edge":
            for c in edge_copy(step[1]):
                c.start()
        else:
            _, name, rel, i = step
            if not got_other:
                own_load.wait()
                for j in range(SPREADS):
                    spread_copy(j).wait_recv()
                got_other = True
            if name == "A":
                task_a(rel, i)
                if i == 2:
                    put(moved("x", rel), 0)
            else:
                part = 2 if name == "B" else 3
                task_bc(part, rel, i)
                if i == 4:
                    for x in range(4):
                        put(x, part)

    for i, x, tiles in queued:
        arrived(i, x, tiles).wait_recv()
    for i, x, tiles in queued:
        local, remote = results(i, x, tiles)
        local.wait()
        remote.wait_send()
    for j in range(SPREADS):
        spread_copy(j).wait_send()
    for m in number:
        message(m, False).wait_send()
    for e, (out, d) in enumerate(((left_out, ahead), (right_out, behind))):
        whole = pltpu.make_async_remote_copy(
            src_ref=panels.at[0, pl.ds(0, EDGE)], dst_ref=out, send_sem=edge_send.at[e], recv_sem=edge_recv.at[e],
            device_id=d, device_id_type=MESH,
        )
        whole.wait_recv()
        whole.wait_send()


def finish_kernel(table, ancestors, y, left, mine, right, diag, off, out, ext, sem):
    u = pl.program_id(0)
    copies = [
        pltpu.make_async_copy(left, ext.at[pl.ds(0, EDGE)], sem.at[0]),
        pltpu.make_async_copy(mine.at[0], ext.at[pl.ds(EDGE, LOCAL)], sem.at[1]),
        pltpu.make_async_copy(right, ext.at[pl.ds(EDGE + LOCAL, EDGE)], sem.at[2]),
    ]

    @pl.when(u == 0)
    def _():
        for c in copies:
            c.start()

    for a in range(ANC):
        off[0, 0, a * B:(a + 1) * B] = -y[0, ancestors[0, table[0, u], a]]

    @pl.when(u == 0)
    def _():
        for c in copies:
            c.wait()

    x = off[0, 0]
    first = u + EDGE - table[1, u]
    for j in range(LOCAL):
        inner = lax.dot_general(ext[first + j], x, (((0,), (0,)), ((), ())), preferred_element_type=F32)
        rows = slice(j * B, (j + 1) * B)
        kept = jnp.where(j < table[2, u], diag[0, 0, rows].astype(F32) - inner, 0.0)
        out[0, 0, rows] = kept.astype(BF16)


def on_device(sep_inv, panels, diag_inverse, widths, ancestors):
    steps = plan()
    sends = sum(s[0] == "send" for s in steps)
    any_space = pl.BlockSpec(memory_space=pl.ANY)
    smem = pl.BlockSpec(memory_space=pltpu.SMEM)
    dma = pltpu.SemaphoreType.DMA
    spread, table = pl.pallas_call(
        spread_kernel,
        name="spread",
        grid=(LOCAL,),
        in_specs=[smem, smem, pl.BlockSpec((1, 1, ANC * B, B), lambda u: (0, u, 0, 0))],
        out_specs=(pl.BlockSpec((CHUNKS, KC, B), lambda u: (0, 0, u)), smem),
        out_shape=(
            jax.ShapeDtypeStruct((CHUNKS, KC, LOCAL * B), BF16),
            jax.ShapeDtypeStruct((3, LOCAL), jnp.int32),
        ),
        scratch_shapes=[pltpu.SMEM((LOCAL, TILES), jnp.int32)],
    )(widths, ancestors, panels)
    y, left, right = pl.pallas_call(
        functools.partial(gather_kernel, steps),
        name="gather",
        out_shape=(
            jax.ShapeDtypeStruct((LOCAL, 8, 4, B, B), BF16),
            jax.ShapeDtypeStruct((EDGE, ANC * B, B), BF16),
            jax.ShapeDtypeStruct((EDGE, ANC * B, B), BF16),
        ),
        in_specs=[any_space, any_space, any_space],
        out_specs=(any_space, any_space, any_space),
        scratch_shapes=[
            pltpu.VMEM((4, 4, 4, 4, B, KC), BF16),
            pltpu.VMEM((CHUNKS, KC, LOCAL * B), BF16),
            pltpu.VMEM((CHUNKS, KC, LOCAL * B), BF16),
            pltpu.VMEM((2, 6, 4 * B, 256), F32),
            pltpu.VMEM((LOCAL, 4, 4, B, B), BF16),
            pltpu.VMEM((LOCAL, 4, 4, B, B), BF16),
            dma((4,)),
            dma,
            dma((sends,)),
            dma((sends,)),
            dma((SPREADS,)),
            dma((SPREADS,)),
            dma((12,)),
            dma((12,)),
            dma((12,)),
            dma((2,)),
            dma((2,)),
        ],
        compiler_params=pltpu.CompilerParams(
            collective_id=0, has_side_effects=True, vmem_limit_bytes=60 * 1024 * 1024
        ),
    )(sep_inv, panels, spread)

    def unit(rows):
        return pl.BlockSpec((1, 1, rows, B), lambda u, *_: (0, u, 0, 0))

    off, diag = pl.pallas_call(
        finish_kernel,
        name="finish",
        grid_spec=pltpu.PrefetchScalarGridSpec(
            num_scalar_prefetch=2,
            grid=(LOCAL,),
            in_specs=[
                pl.BlockSpec((1, TILES, B, B), lambda u, *_: (u, 0, 0, 0)),
                any_space, any_space, any_space, unit(LOCAL * B),
            ],
            out_specs=[unit(ANC * B), unit(LOCAL * B)],
            scratch_shapes=[pltpu.VMEM((2 * EDGE + LOCAL, ANC * B, B), BF16), dma((3,))],
        ),
        out_shape=(
            jax.ShapeDtypeStruct((1, LOCAL, ANC * B, B), BF16),
            jax.ShapeDtypeStruct((1, LOCAL, LOCAL * B, B), BF16),
        ),
        compiler_params=pltpu.CompilerParams(vmem_limit_bytes=40 * 1024 * 1024),
    )(table, ancestors, y.reshape(LOCAL, TILES, B, B), left, panels, right, diag_inverse)
    return off, diag


def solution(mesh):
    placed = (
        P("grp", "dev"),
        P("grp", "dev", None, None),
        P("grp", "dev", None, None),
        P("grp", None),
        P("grp", None, None),
    )
    return jax.shard_map(
        on_device,
        mesh=mesh,
        in_specs=placed,
        out_specs=(P("grp", "dev", None, None), P("grp", "dev", None, None)),
        check_vma=False,
    )
```

time: 492 us -> 157 us (0.32)
  the two profiles are of different devices: /device:TPU:1 before, /device:TPU:22 now
where the time goes in v1:
time: 157 us; the launch traced here: 156 us
  Pallas kernels  149 us (95%)
  local copies, waits for them, and re-layouts  6.13 us (4%)
    pallas_call x1, Pallas kernels, on_device(): pl.pallas_call(functools.partial(gather_kernel, steps), name='gather', ou...  131 us
    pallas_call x1, Pallas kernels, on_device(): pl.pallas_call(finish_kernel, name='finish', grid_spec=pltpu.PrefetchScal...  10.5 us
    pallas_call x1, Pallas kernels, on_device(): pl.pallas_call(spread_kernel, name='spread', grid=(LOCAL,), in_specs=[sme...  7.85 us
    unnamed x13, local copies, waits for them, and re-layouts  6.13 us

profile of v1, /device:TPU:22, one launch (start us, length us, event | category | flops | bytes accessed | tf_op | source)
XLA Modules:
  0.0 156.1 jit_solution(17968725527119056337)
XLA Ops:
  0.6 1.4 copy.7.ancestors
  2.0 7.9 %spread.1 = (bf16[16,256,768]{2,1,0:T(8,128)(2,1)}, s32[3,6]{1,0:T(4,128)}) custom-call(s32[1,32]{1,0:T(1,128)} %widths.1, s32[1,32,16]{2,1,0:T(8,128)} %copy.7.ancestors, bf16[1,6,2048,128]{3,2,1,0:T(8,128)(2,1)} %mine.1), custom_call_target="tpu_custom_call" | custom-call | tf_op jit(solution)/shard_map/spread/pallas_call | solution.py:375
  9.9 0.0 copy-start
  9.9 0.0 copy-start.4
  9.9 0.0 copy-start.5
  9.9 130.7 %gather.1 = (bf16[6,8,4,128,128]{4,3,2,1,0:T(8,128)(2,1)}, bf16[5,2048,128]{2,1,0:T(8,128)(2,1)}, bf16[5,2048,128]{2,1,0:T(8,128)(2,1)}) custom-call(bf16[512,256]{1,0:T(8,128)(2,1)} %sep.1, bf16[1,6,2048,128]{3,2,1,0:T(8,128)(2,1)} %mine.1, bf16[16,256,768]{2,1,0:T(8,128)(2,1)} %get-tuple-element.8.spread), custom_call_target="tpu_custom_call" | custom-call | tf_op jit(solution)/shard_map/gather/pallas_call | solution.py:387
  140.6 0.0 copy-done
  140.6 0.0 copy-done.4
  140.6 0.0 copy-done.5
  140.6 0.0 copy-start.1
  140.6 1.7 %copy-done.1 = bf16[5,2048,128]{2,1,0:T(8,128)(2,1)S(1)} copy-done((bf16[5,2048,128]{2,1,0:T(8,128)(2,1)S(1)}, bf16[5,2048,128]{2,1,0:T(8,128)(2,1)}, u32[]{:S(2)}) %copy-start.1) | copy-done | bytes 2621464
  142.3 0.0 copy-start.2
  142.3 1.7 %copy-done.2 = bf16[5,2048,128]{2,1,0:T(8,128)(2,1)S(1)} copy-done((bf16[5,2048,128]{2,1,0:T(8,128)(2,1)S(1)}, bf16[5,2048,128]{2,1,0:T(8,128)(2,1)}, u32[]{:S(2)}) %copy-start.2) | copy-done | bytes 2621464
  144.1 0.0 copy-start.3
  144.1 1.3 copy-done.3
  145.4 10.5 %finish.1 = (bf16[1,6,2048,128]{3,2,1,0:T(8,128)(2,1)}, bf16[1,6,768,128]{3,2,1,0:T(8,128)(2,1)}) custom-call(s32[3,6]{1,0:T(4,128)S(1)} %copy-done.5, s32[1,32,16]{2,1,0:T(8,128)S(1)} %copy-done.4, bf16[6,32,128,128]{3,2,1,0:T(8,128)(2,1)} %bitcast.1, bf16[5,2048,128]{2,1,0:T(8,128)(2,1)S(1)} %copy-done.1, bf16[1,6,2048,128]{3,2,1,0:T(8,128)(2,1)S(1)} %copy-done, ...), custom_call_target="tpu_custom_call" | custom-call | tf_op jit(solution)/shard_map/finish/pallas_call | solution.py:424
Async XLA Ops:
  9.9 130.7 %copy-start = (bf16[1,6,2048,128]{3,2,1,0:T(8,128)(2,1)S(1)}, bf16[1,6,2048,128]{3,2,1,0:T(8,128)(2,1)}, u32[]{:S(2)}) copy-start(bf16[1,6,2048,128]{3,2,1,0:T(8,128)(2,1)} %mine.1) | copy-start | bytes 9437188
  9.9 130.7 %copy-start.4 = (s32[1,32,16]{2,1,0:T(8,128)S(1)}, s32[1,32,16]{2,1,0:T(8,128)}, u32[]{:S(2)}) copy-start(s32[1,32,16]{2,1,0:T(8,128)} %copy.7.ancestors) | copy-start | bytes 6148
  9.9 130.7 %copy-start.5 = (s32[3,6]{1,0:T(4,128)S(1)}, s32[3,6]{1,0:T(4,128)}, u32[]{:S(2)}) copy-start(s32[3,6]{1,0:T(4,128)} %get-tuple-element.7.table) | copy-start | bytes 220
  140.6 1.7 %copy-start.1 = (bf16[5,2048,128]{2,1,0:T(8,128)(2,1)S(1)}, bf16[5,2048,128]{2,1,0:T(8,128)(2,1)}, u32[]{:S(2)}) copy-start(bf16[5,2048,128]{2,1,0:T(8,128)(2,1)} %get-tuple-element.10.left) | copy-start | bytes 7864324
  142.3 1.7 %copy-start.2 = (bf16[5,2048,128]{2,1,0:T(8,128)(2,1)S(1)}, bf16[5,2048,128]{2,1,0:T(8,128)(2,1)}, u32[]{:S(2)}) copy-start(bf16[5,2048,128]{2,1,0:T(8,128)(2,1)} %get-tuple-element.11.right) | copy-start | bytes 7864324
  144.1 1.3 copy-start.3

commit v2 on v1

v2 whole, which is shorter than its diff:
```python
import functools
import heapq

import jax
import jax.numpy as jnp
from jax import lax
from jax.experimental import pallas as pl
from jax.experimental.pallas import tpu as pltpu
from jax.sharding import PartitionSpec as P

MESH = pl.DeviceIdType.MESH
F32 = jnp.float32
BF16 = jnp.bfloat16
PARTS = (
    (0, 0, 128, ("y", "z", "x")),
    (1, 0, 128, ("z", "y", "x")),
    (2, 0, 128, ("z", "x", "y")),
    (3, 0, 64, ("z", "x", "y")),
    (3, 64, 64, ("y", "x", "z")),
)
ORDER = tuple(p[3] for p in PARTS)
B = 128
LOCAL = 6
EDGE = 5
ANC = 16
TILES = 32
NSG = 32
CHUNKS = 16
KC = 256
SPREADS = 8
HALOS = 20


def plan():
    rate, latency, depth, edge = 42e3, 2.5, 4.0, 512 * B * 2
    steps, heap, got, held = [], [], {"edges": 0}, {2: [], 3: [], 4: []}
    queue = {(axis, s): [] for axis in ("x", "y", "z") for s in (1, -1)}
    free = {link: 0.0 for link in queue}
    tasks = [("spread", 0, i) for i in range(SPREADS)]
    clock = 0.0
    cost = {"spread": 0.5, "A": 1.25, "far": 0.95, "plane": 1.7, "group": 0.9}

    def send(m):
        part, phase, a, s, kind = m
        link = (ORDER[part][phase - 1], s)
        heapq.heappush(queue[link], (phase, kind == "half", len(steps), count("sent"), m))

    def pump():
        for link, waiting in queue.items():
            while waiting and free[link] < clock + depth:
                m = heapq.heappop(waiting)[4]
                size = PARTS[m[0]][2] * KC * 2 * (4 if m[1] == 3 else 1) // (2 if m[4] == "half" else 1)
                free[link] = max(clock, free[link]) + size / rate
                heapq.heappush(heap, (free[link] + latency, count("event"), m))
                steps.append(("send", m))
        while count("pump") and got["edges"] < HALOS and not queue["z", 1] and free["z", 1] < clock + depth:
            i = got["edges"]
            got["edges"] += 1
            for s in (1, -1):
                free["z", s] = max(clock, free["z", s]) + edge / rate
            steps.append(("edge", i))
            if i % 2:
                heapq.heappush(heap, (free["z", 1] + 2 * latency, count("event"), ("edge", i)))

    def near(part, phase, a):
        for s in (1, -1):
            send((part, phase, a, s, "near"))

    def count(key):
        got[key] = got.get(key, 0) + 1
        return got[key]

    def plane(part, rel):
        if part < 2:
            if count(("A", rel)) == 8:
                tasks.extend(("A", rel, i) for i in range(3))
        elif count((part, "plane", rel)) == 4:
            tasks.append(("plane", part, rel, count((part, "order"))))
            if got[(part, "order")] == 3:
                tasks.extend(held[part])

    def far(part, a):
        if part < 2:
            tasks.append(("far", part, a, count(("far", part))))
        else:
            group = ("group", part, a)
            (tasks if got.get((part, "order"), 0) == 3 else held[part]).append(group)

    def handle(m):
        part, phase, a, s, kind = m
        if phase == 1:
            if kind == "near":
                send((part, 1, 0, s, "half"))
                near(part, 2, -s)
                full = count((part, 1))
            elif count((part, 1, "far")) == 2:
                near(part, 2, 2)
                full = count((part, 1))
            else:
                full = 0
            if full == 3:
                near(part, 3, 0)
                plane(part, 0)
        elif phase == 2:
            if kind == "near":
                send((part, 2, a, s, "half"))
                if count((part, 2, -s)) == 4:
                    near(part, 3, -s)
                    plane(part, 0)
            elif count((part, 2, 2)) == 8:
                near(part, 3, 2)
                plane(part, 0)
        elif kind == "near":
            send((part, 3, a, s, "half"))
            plane(part, -s)
        elif count((part, 3, a, "far")) == 2:
            far(part, a)

    for phase in (1, 2):
        for part in range(len(PARTS)):
            near(part, phase, 0)
    pump()
    while heap or tasks or got["edges"] < HALOS:
        while heap and heap[0][0] <= clock:
            m = heapq.heappop(heap)[2]
            if m[0] == "edge":
                steps.append(("forward", m[1]))
                for s in (1, -1):
                    free["y", s] = max(clock, free["y", s]) + edge / rate
            else:
                steps.append(("wait", m))
                handle(m)
        pump()
        if tasks:
            task = tasks.pop(0)
            steps.append(("task",) + task)
            clock += cost[task[0]]
        elif heap:
            clock = max(clock, heap[0][0])
        else:
            clock += 1.0
    return steps


def spans(widths, position):
    def step(k, carry):
        end, owner, start, width = carry
        w = widths[0, k]
        inside = [(position + u >= end) & (position + u < end + w) for u in range(LOCAL)]
        owner = tuple(jnp.where(i, k, o) for i, o in zip(inside, owner))
        start = tuple(jnp.where(i, end, o) for i, o in zip(inside, start))
        width = tuple(jnp.where(i, w, o) for i, o in zip(inside, width))
        return end + w, owner, start, width

    zeros = (jnp.int32(0),) * LOCAL
    _, owner, start, width = lax.fori_loop(0, NSG, step, (jnp.int32(0), zeros, zeros, zeros))
    return owner, start, width


def table_kernel(widths, ancestors, table, spot):
    owner, start, width = spans(widths, lax.axis_index("dev") * LOCAL)
    for v in range(LOCAL):
        table[0, v] = owner[v]
        table[1, v] = lax.axis_index("dev") * LOCAL + v - start[v]
        table[2, v] = width[v]
        for t in range(TILES):
            spot[v, t] = ANC
        for a in range(ANC):
            spot[v, ancestors[0, owner[v], a]] = a


def gather_kernel(
    steps, sep, panels, spot, y_out, left_out, right_out, left_on, right_on,
    blocks, own, other, total, last, stage_own, stage_other, pan,
    load_sem, pan_sem, send_sem, recv_sem, half_send, half_recv, y_local, y_send, y_recv, edge_send, edge_recv,
    hop_send, hop_recv, on_send, on_recv,
):
    grp, dev = lax.axis_index("grp"), lax.axis_index("dev")
    core = lax.rem(grp, 2)
    at = {"x": grp // 2, "y": dev // 4, "z": lax.rem(dev, 4)}

    def moved(axis, by):
        return lax.rem(at[axis] + by + 4, 4)

    def device(axis, by):
        to = dict(at)
        to[axis] = moved(axis, by)
        return (to["x"] * 2 + core, to["y"] * 4 + to["z"])

    partner = (at["x"] * 2 + 1 - core, dev)
    ahead, behind = (grp, lax.rem(dev + 1, 16)), (grp, lax.rem(dev + 15, 16))

    loads = [
        pltpu.make_async_copy(
            sep.at[pl.ds(p * B, B)], blocks.at[p, at["x"], at["y"], at["z"]], load_sem.at[p]
        )
        for p in range(4)
    ]
    pan_load = pltpu.make_async_copy(panels.at[0], pan.at[:, pl.ds(0, ANC)], pan_sem)
    for c in loads:
        c.start()
    pan_load.start()
    pan[:, ANC] = jnp.zeros((LOCAL, B, B), BF16)
    barrier = pltpu.get_barrier_semaphore()
    greeted = [device(a, s) for a in ("x", "y", "z") for s in (1, -1)] + [partner, ahead, behind]
    for d in greeted:
        pl.semaphore_signal(barrier, inc=1, device_id=d, device_id_type=MESH)
    for c in loads:
        c.wait()
    pl.semaphore_wait(barrier, len(greeted))

    number = {m: i for i, m in enumerate(s[1] for s in steps if s[0] == "send")}

    def message(m, arriving):
        part, phase, a, s, kind = m
        axes = ORDER[part]
        axis = axes[phase - 1]
        row, low, rows, _ = PARTS[part]
        where = dict(at)
        if phase == 2:
            where[axes[0]] = moved(axes[0], a)
        if phase == 3:
            where[axes[0]] = slice(None)
            where[axes[1]] = moved(axes[1], a)
        gone = (0 if kind == "near" else 1) + (1 if arriving else 0)
        where[axis] = moved(axis, -s * gone)
        columns = slice(None) if kind == "near" else pl.ds(0 if s == 1 else B, B)
        ref = blocks.at[row, where["x"], where["y"], where["z"], pl.ds(low, rows), columns]
        return pltpu.make_async_remote_copy(
            src_ref=ref, dst_ref=ref, send_sem=send_sem.at[number[m]], recv_sem=recv_sem.at[number[m]],
            device_id=device(axis, s), device_id_type=MESH,
        )

    def spread_copy(i):
        some = pl.ds(CHUNKS // SPREADS * i, CHUNKS // SPREADS)
        return pltpu.make_async_remote_copy(
            src_ref=own.at[some], dst_ref=other.at[some], send_sem=half_send.at[i], recv_sem=half_recv.at[i],
            device_id=partner, device_id_type=MESH,
        )

    def edge_copy(i):
        t, rows = i // 4, pl.ds((i % 4) * 4, 4)
        sides = ((panels.at[0, LOCAL - EDGE + t, rows], left_out, ahead, 1), (panels.at[0, t, rows], right_out, behind, -1))
        return [
            pltpu.make_async_remote_copy(
                src_ref=src, dst_ref=out.at[t, rows],
                send_sem=hop_send.at[e, i // 2] if i % 2 else edge_send.at[e],
                recv_sem=hop_recv.at[e, i // 2] if i % 2 else edge_recv.at[e],
                device_id=device("z", s) if i % 2 else d, device_id_type=MESH,
            )
            for e, (src, out, d, s) in enumerate(sides)
        ]

    def edge_on(i):
        t, rows = i // 4, pl.ds((i % 4) * 4, 4)
        return [
            (at["z"] == z, pltpu.make_async_remote_copy(
                src_ref=out.at[t, rows], dst_ref=on.at[t, rows], send_sem=on_send.at[e, i // 2],
                recv_sem=on_recv.at[e, i // 2], device_id=device("y", s), device_id_type=MESH,
            ))
            for e, (out, on, z, s) in enumerate(((left_out, left_on, 0, 1), (right_out, right_on, 3, -1)))
        ]

    def results(i, x, tiles):
        here, there = pl.ds(tiles, 2 if tiles == 0 else 1), 2 * x + core
        return (
            pltpu.make_async_copy(stage_own.at[:, x, here], y_out.at[:, there, here], y_local.at[i]),
            pltpu.make_async_remote_copy(
                src_ref=stage_other.at[:, x, here], dst_ref=y_out.at[:, there, here],
                send_sem=y_send.at[i], recv_sem=y_recv.at[i], device_id=partner, device_id_type=MESH,
            ),
        )

    def arrived(i, x, tiles):
        here, there = pl.ds(tiles, 2 if tiles == 0 else 1), 2 * x + 1 - core
        return pltpu.make_async_remote_copy(
            src_ref=y_out.at[:, there, here], dst_ref=y_out.at[:, there, here],
            send_sem=y_send.at[i], recv_sem=y_recv.at[i], device_id=partner, device_id_type=MESH,
        )

    queued = []

    def put(x, tiles):
        i = len(queued)
        queued.append((i, x, tiles))
        for c in results(i, x, tiles):
            c.start()

    sides = ((own, stage_own), (other, stage_other))

    def keep(stage, n, x, part, value):
        row, low, rows, _ = part
        for v in range(2):
            stage[2 * n + v, x, row, low:low + rows] = value[:, v * B:(v + 1) * B]

    def task_a(rel, n):
        x = moved("x", rel)
        cols = pl.ds(n * 256, 256)
        for source, stage in sides:
            acc = jnp.zeros((2 * B, 256), F32)
            for k in range(CHUNKS):
                lhs = blocks[0:2, x, k // 4, k % 4].reshape(2 * B, KC)
                acc = acc + jnp.dot(lhs, source[k, :, cols], preferred_element_type=F32)
            value = acc.astype(BF16)
            for p in range(2):
                keep(stage, n, x, PARTS[p], value[p * B:(p + 1) * B])

    def columns(body):
        def column(n, carry):
            for h, (source, stage) in enumerate(sides):
                body(n, pl.ds(pl.multiple_of(n * 256, 256), 256), 3 * h + n, source, stage)
            return carry

        lax.fori_loop(0, 3, column, 0)

    def task_far(part, a, nth):
        x, fixed = moved("x", 2), moved(ORDER[part][1], a)

        def body(n, cols, slot, source, stage):
            acc = jnp.zeros((B, 256), F32)
            for k in range(4):
                y, z = (k, fixed) if part == 0 else (fixed, k)
                acc = acc + jnp.dot(blocks[part, x, y, z], source[y * 4 + z, :, cols], preferred_element_type=F32)
            if nth > 1:
                acc = acc + last[part, slot]
            if nth < 4:
                last[part, slot] = acc
            else:
                keep(stage, n, x, PARTS[part], acc.astype(BF16))

        columns(body)

    def tile_of(part, fixed, k):
        return (fixed, k) if ORDER[part][2] == "y" else (k, fixed)

    def some(part):
        row, low, rows, _ = PARTS[part]
        return row, pl.ds(low, rows), rows

    def task_plane(part, rel, nth):
        row, span, rows = some(part)
        fixed = moved(ORDER[part][2], rel)

        def body(n, cols, slot, source, stage):
            acc = jnp.zeros((4 * rows, 256), F32)
            for k in range(4):
                y, z = tile_of(part, fixed, k)
                lhs = blocks[row, :, y, z, span].reshape(4 * rows, KC)
                acc = acc + jnp.dot(lhs, source[y * 4 + z, :, cols], preferred_element_type=F32)
            if nth > 1:
                acc = acc + total[row - 2, slot, :, span].reshape(4 * rows, 256)
            total[row - 2, slot, :, span] = acc.reshape(4, rows, 256)

        columns(body)

    def task_group(part, a):
        row, span, rows = some(part)
        fixed, x = moved(ORDER[part][2], 2), moved("x", a)

        def body(n, cols, slot, source, stage):
            acc = total[row - 2, slot, x, span]
            for k in range(4):
                y, z = tile_of(part, fixed, k)
                acc = acc + jnp.dot(blocks[row, x, y, z, span], source[y * 4 + z, :, cols], preferred_element_type=F32)
            keep(stage, n, x, PARTS[part], acc.astype(BF16))

        columns(body)

    def spread(i):
        for j in range(4):
            t = 4 * i + j
            for u in range(LOCAL):
                own[t // 2, (t % 2) * B:(t % 2 + 1) * B, u * B:(u + 1) * B] = pan[u, spot[u, t]]

    got_other, ended = False, {}
    for step in steps:
        if step[0] == "send":
            message(step[1], False).start()
        elif step[0] == "wait":
            message(step[1], True).wait_recv()
        elif step[0] == "edge":
            for c in edge_copy(step[1]):
                c.start()
        elif step[0] == "forward":
            for c in edge_copy(step[1]):
                c.wait_recv()
            for c_if, c in edge_on(step[1]):
                pl.when(c_if)(c.start)
        else:
            name = step[1]
            if name == "spread":
                i = step[3]
                if i == 0:
                    pan_load.wait()
                spread(i)
                if i > 0:
                    spread_copy(i - 1).start()
                continue
            if not got_other:
                spread_copy(SPREADS - 1).start()
                for j in range(SPREADS):
                    spread_copy(j).wait_recv()
                got_other = True
            if name == "A":
                task_a(step[2], step[3])
                if step[3] == 2:
                    put(moved("x", step[2]), 0)
            elif name == "far":
                task_far(*step[2:])
                ended["far"] = ended.get("far", 0) + 1
                if ended["far"] == 8:
                    put(moved("x", 2), 0)
            elif name == "plane":
                task_plane(*step[2:])
            else:
                task_group(*step[2:])
                key = (PARTS[step[2]][0], step[3])
                ended[key] = ended.get(key, 0) + PARTS[step[2]][2]
                if ended[key] == B:
                    put(moved("x", step[3]), key[0])

    for i, x, tiles in queued:
        arrived(i, x, tiles).wait_recv()
    for i, x, tiles in queued:
        local, remote = results(i, x, tiles)
        local.wait()
        remote.wait_send()
    for j in range(SPREADS):
        spread_copy(j).wait_send()
    for m in number:
        message(m, False).wait_send()
    for i in range(1, HALOS, 2):
        for c in edge_copy(i):
            c.wait_send()
        for c_if, c in edge_on(i):
            pl.when(c_if)(c.wait)
    for e, (out, d) in enumerate(((left_out, ahead), (right_out, behind))):
        whole = pltpu.make_async_remote_copy(
            src_ref=panels.at[0, pl.ds(0, EDGE), pl.ds(0, ANC // 2)], dst_ref=out.at[:, pl.ds(0, ANC // 2)],
            send_sem=edge_send.at[e], recv_sem=edge_recv.at[e], device_id=d, device_id_type=MESH,
        )
        whole.wait_recv()
        whole.wait_send()


def finish_kernel(table, ancestors, y, left, mine, right, left_on, right_on, diag, off, out, ext, rows, ext_sem, row_sem):
    u = pl.program_id(0)
    z = lax.rem(lax.axis_index("dev"), 4)

    def pieces(source, first, e):
        return [
            pltpu.make_async_copy(
                source.at[:, pl.ds(4 * q, 4)], ext.at[pl.ds(first, EDGE), pl.ds(4 * q, 4)], ext_sem.at[e, q]
            )
            for q in range(4)
        ]

    middle = pltpu.make_async_copy(mine.at[0], ext.at[pl.ds(EDGE, LOCAL)], ext_sem.at[2, 0])
    edges = [
        (pieces(left, 0, 0), pieces(left_on, 0, 0), z == 0),
        (pieces(right, EDGE + LOCAL, 1), pieces(right_on, EDGE + LOCAL, 1), z == 3),
    ]

    row_copies = [pltpu.make_async_copy(y.at[v], rows.at[v], row_sem.at[v]) for v in range(LOCAL)]

    @pl.when(u == 0)
    def _():
        row_copies[0].start()
        middle.start()
        for near, far, crossed in edges:
            for q in range(4):
                if q % 2:
                    pl.when(crossed)(far[q].start)
                    pl.when(jnp.logical_not(crossed))(near[q].start)
                else:
                    near[q].start()
        for c in row_copies[1:]:
            c.start()

    pltpu.make_async_copy(y.at[u], rows.at[u], row_sem.at[u]).wait()
    for a in range(ANC):
        off[0, 0, a * B:(a + 1) * B] = -rows[u, ancestors[0, table[0, u], a]]
    x = off[0, 0].T

    @pl.when(u == 0)
    def _():
        middle.wait()
        for near, _, _ in edges:
            for c in near:
                c.wait()

    first = u + EDGE - table[1, u]
    for j in range(0, LOCAL, 2):
        pair = jnp.concatenate([ext[first + j].reshape(ANC * B, B), ext[first + j + 1].reshape(ANC * B, B)], axis=1)
        inner = jnp.dot(x, pair, preferred_element_type=F32)
        for v in range(2):
            at = slice((j + v) * B, (j + v + 1) * B)
            kept = diag[0, 0, at].astype(F32) - inner[:, v * B:(v + 1) * B].T
            out[0, 0, at] = jnp.where(j + v < table[2, u], kept, 0.0).astype(BF16)


def on_device(sep_inv, panels, diag_inverse, widths, ancestors):
    steps = plan()
    sends = sum(s[0] == "send" for s in steps)
    any_space = pl.BlockSpec(memory_space=pl.ANY)
    smem = pl.BlockSpec(memory_space=pltpu.SMEM)
    dma = pltpu.SemaphoreType.DMA
    hbm = pl.BlockSpec(memory_space=pltpu.HBM)
    tiled = panels.reshape(1, LOCAL, ANC, B, B)
    table, spot = pl.pallas_call(
        table_kernel,
        name="table",
        in_specs=[smem, smem],
        out_specs=(smem, smem),
        out_shape=(jax.ShapeDtypeStruct((3, LOCAL), jnp.int32), jax.ShapeDtypeStruct((LOCAL, TILES), jnp.int32)),
    )(widths, ancestors)
    y, left, right, left_on, right_on = pl.pallas_call(
        functools.partial(gather_kernel, steps),
        name="gather",
        out_shape=(
            jax.ShapeDtypeStruct((LOCAL, 8, 4, B, B), BF16),
        ) + (jax.ShapeDtypeStruct((EDGE, ANC, B, B), BF16),) * 4,
        in_specs=[any_space, any_space, smem],
        out_specs=(hbm,) * 5,
        scratch_shapes=[
            pltpu.VMEM((4, 4, 4, 4, B, KC), BF16),
            pltpu.VMEM((CHUNKS, KC, LOCAL * B), BF16),
            pltpu.VMEM((CHUNKS, KC, LOCAL * B), BF16),
            pltpu.VMEM((2, 6, 4, B, 256), F32),
            pltpu.VMEM((2, 6, B, 256), F32),
            pltpu.VMEM((LOCAL, 4, 4, B, B), BF16),
            pltpu.VMEM((LOCAL, 4, 4, B, B), BF16),
            pltpu.VMEM((LOCAL, ANC + 1, B, B), BF16),
            dma((4,)),
            dma,
            dma((sends,)),
            dma((sends,)),
            dma((SPREADS,)),
            dma((SPREADS,)),
            dma((12,)),
            dma((12,)),
            dma((12,)),
            dma((2,)),
            dma((2,)),
            dma((2, HALOS // 2)),
            dma((2, HALOS // 2)),
            dma((2, HALOS // 2)),
            dma((2, HALOS // 2)),
        ],
        compiler_params=pltpu.CompilerParams(
            collective_id=0, has_side_effects=True, vmem_limit_bytes=60 * 1024 * 1024
        ),
    )(sep_inv, tiled, spot)

    def unit(rows):
        return pl.BlockSpec((1, 1, rows, B), lambda u, *_: (0, u, 0, 0))

    off, diag = pl.pallas_call(
        finish_kernel,
        name="finish",
        grid_spec=pltpu.PrefetchScalarGridSpec(
            num_scalar_prefetch=2,
            grid=(LOCAL,),
            in_specs=[
                hbm, hbm, hbm, hbm, hbm, hbm, unit(LOCAL * B),
            ],
            out_specs=[unit(ANC * B), unit(LOCAL * B)],
            scratch_shapes=[
                pltpu.VMEM((2 * EDGE + LOCAL, ANC, B, B), BF16),
                pltpu.VMEM((LOCAL, TILES, B, B), BF16),
                dma((3, 4)),
                dma((LOCAL,)),
            ],
        ),
        out_shape=(
            jax.ShapeDtypeStruct((1, LOCAL, ANC * B, B), BF16),
            jax.ShapeDtypeStruct((1, LOCAL, LOCAL * B, B), BF16),
        ),
        compiler_params=pltpu.CompilerParams(vmem_limit_bytes=62 * 1024 * 1024),
    )(table, ancestors, y.reshape(LOCAL, TILES, B, B), left, tiled, right, left_on, right_on, diag_inverse)
    return off, diag


def solution(mesh):
    placed = (
        P("grp", "dev"),
        P("grp", "dev", None, None),
        P("grp", "dev", None, None),
        P("grp", None),
        P("grp", None, None),
    )
    return jax.shard_map(
        on_device,
        mesh=mesh,
        in_specs=placed,
        out_specs=(P("grp", "dev", None, None), P("grp", "dev", None, None)),
        check_vma=False,
    )
```

time: 157 us -> 135 us (0.86)
  the two profiles are of different devices: /device:TPU:22 before, /device:TPU:1 now
where the time goes in v2:
time: 135 us; the launch traced here: 134 us
  Pallas kernels  132 us (98%)
  local copies, waits for them, and re-layouts  1.37 us (1%)
    pallas_call x1, Pallas kernels, on_device(): pl.pallas_call(functools.partial(gather_kernel, steps), name='gather', ou...  116 us
    pallas_call x1, Pallas kernels, on_device(): pl.pallas_call(finish_kernel, name='finish', grid_spec=pltpu.PrefetchScal...  13.3 us
    pallas_call x1, Pallas kernels, on_device(): pl.pallas_call(table_kernel, name='table', in_specs=[smem, smem], out_spe...  2.78 us

profile of v2, /device:TPU:1, one launch (start us, length us, event | category | flops | bytes accessed | tf_op | source)
XLA Modules:
  0.0 133.9 jit_solution(1198673441064765643)
XLA Ops:
  0.6 1.4 %copy.7.ancestors = s32[1,32,16]{2,1,0:T(8,128)} copy(s32[1,32,16]{1,2,0:T(8,128)} %param.9) | data formatting | bytes 4096 | tf_op args[4]
  2.0 2.8 %table.1 = (s32[3,6]{1,0:T(4,128)}, s32[6,32]{1,0:T(8,128)}) custom-call(s32[1,32]{1,0:T(1,128)} %widths.1, s32[1,32,16]{2,1,0:T(8,128)} %copy.7.ancestors), custom_call_target="tpu_custom_call" | custom-call | tf_op jit(solution)/shard_map/table/pallas_call | solution.py:510
  4.8 115.7 %gather.1 = (bf16[6,8,4,128,128]{4,3,2,1,0:T(8,128)(2,1)}, bf16[5,16,128,128]{3,2,1,0:T(8,128)(2,1)}, bf16[5,16,128,128]{3,2,1,0:T(8,128)(2,1)}, bf16[5,16,128,1...) custom-call(bf16[512,256]{1,0:T(8,128)(2,1)} %sep.1, bf16[1,6,16,128,128]{4,3,2,1,0:T(8,128)(2,1)} %bitcast.2, ...), custom_call_target="tpu_custom_call" | custom-call | tf_op jit(solution)/shard_map/gather/pallas_call | solution.py:517
  120.5 13.3 %finish.1 = (bf16[1,6,2048,128]{3,2,1,0:T(8,128)(2,1)}, bf16[1,6,768,128]{3,2,1,0:T(8,128)(2,1)}) custom-call(s32[3,6]{1,0:T(4,128)} %get-tuple-element.9.table, s32[1,32,16]{2,1,0:T(8,128)} %copy.7.ancestors, bf16[6,32,128,128]{3,2,1,0:T(8,128)(2,1)} %bitcast.4, bf16[5,16,128,128]{3,2,1,0:T(8,128)(2,1)} %get-tuple-element.12.left, ...), custom_call_target="tpu_custom_call" | custom-call | tf_op jit(solution)/shard_map/finish/pallas_call | solution.py:558

commit v3 on v2

--- a/solution.py
+++ b/solution.py
@@ -142,31 +142,32 @@
     return steps
 
 
-def spans(widths, position):
-    def step(k, carry):
-        end, owner, start, width = carry
+def spans(widths, position, table):
+    def step(k, end):
         w = widths[0, k]
-        inside = [(position + u >= end) & (position + u < end + w) for u in range(LOCAL)]
-        owner = tuple(jnp.where(i, k, o) for i, o in zip(inside, owner))
-        start = tuple(jnp.where(i, end, o) for i, o in zip(inside, start))
-        width = tuple(jnp.where(i, w, o) for i, o in zip(inside, width))
-        return end + w, owner, start, width
-
-    zeros = (jnp.int32(0),) * LOCAL
-    _, owner, start, width = lax.fori_loop(0, NSG, step, (jnp.int32(0), zeros, zeros, zeros))
-    return owner, start, width
+
+        @pl.when((end < position + LOCAL) & (end + w > position))
+        def _():
+            for u in range(LOCAL):
+                @pl.when((position + u >= end) & (position + u < end + w))
+                def _():
+                    table[0, u] = k
+                    table[1, u] = position + u - end
+                    table[2, u] = w
+
+        return end + w
+
+    lax.fori_loop(0, NSG, step, jnp.int32(0))
 
 
 def table_kernel(widths, ancestors, table, spot):
-    owner, start, width = spans(widths, lax.axis_index("dev") * LOCAL)
+    spans(widths, lax.axis_index("dev") * LOCAL, table)
     for v in range(LOCAL):
-        table[0, v] = owner[v]
-        table[1, v] = lax.axis_index("dev") * LOCAL + v - start[v]
-        table[2, v] = width[v]
+        owner = table[0, v]
         for t in range(TILES):
             spot[v, t] = ANC
         for a in range(ANC):
-            spot[v, ancestors[0, owner[v], a]] = a
+            spot[v, ancestors[0, a, owner]] = a
 
 
 def gather_kernel(
@@ -254,12 +255,18 @@
     def edge_on(i):
         t, rows = i // 4, pl.ds((i % 4) * 4, 4)
         return [
-            (at["z"] == z, pltpu.make_async_remote_copy(
+            pltpu.make_async_remote_copy(
                 src_ref=out.at[t, rows], dst_ref=on.at[t, rows], send_sem=on_send.at[e, i // 2],
                 recv_sem=on_recv.at[e, i // 2], device_id=device("y", s), device_id_type=MESH,
-            ))
-            for e, (out, on, z, s) in enumerate(((left_out, left_on, 0, 1), (right_out, right_on, 3, -1)))
+            )
+            for e, (out, on, s) in enumerate(((left_out, left_on, 1), (right_out, right_on, -1)))
         ]
+
+    last_dev = 15
+    sends_edge, takes_edge = (dev < last_dev, dev > 0), (dev > 0, dev < last_dev)
+    first_z, last_z = at["z"] == 0, at["z"] == 3
+    sends_on = (first_z & (at["y"] < 3), last_z & (at["y"] > 0))
+    takes_on = (first_z & (at["y"] > 0), last_z & (at["y"] < 3))
 
     def results(i, x, tiles):
         here, there = pl.ds(tiles, 2 if tiles == 0 else 1), 2 * x + core
@@ -379,13 +386,16 @@
         elif step[0] == "wait":
             message(step[1], True).wait_recv()
         elif step[0] == "edge":
-            for c in edge_copy(step[1]):
-                c.start()
+            for c, sends in zip(edge_copy(step[1]), sends_edge):
+                if step[1] % 2:
+                    c.start()
+                else:
+                    pl.when(sends)(c.start)
         elif step[0] == "forward":
             for c in edge_copy(step[1]):
                 c.wait_recv()
-            for c_if, c in edge_on(step[1]):
-                pl.when(c_if)(c.start)
+            for c, sends in zip(edge_on(step[1]), sends_on):
+                pl.when(sends)(c.start)
         else:
             name = step[1]
             if name == "spread":
@@ -432,62 +442,70 @@
     for i in range(1, HALOS, 2):
         for c in edge_copy(i):
             c.wait_send()
-        for c_if, c in edge_on(i):
-            pl.when(c_if)(c.wait)
+        for c, sends, takes in zip(edge_on(i), sends_on, takes_on):
+            pl.when(sends)(c.wait_send)
+            pl.when(takes)(c.wait_recv)
     for e, (out, d) in enumerate(((left_out, ahead), (right_out, behind))):
         whole = pltpu.make_async_remote_copy(
             src_ref=panels.at[0, pl.ds(0, EDGE), pl.ds(0, ANC // 2)], dst_ref=out.at[:, pl.ds(0, ANC // 2)],
             send_sem=edge_send.at[e], recv_sem=edge_recv.at[e], device_id=d, device_id_type=MESH,
         )
-        whole.wait_recv()
-        whole.wait_send()
+        pl.when(takes_edge[e])(whole.wait_recv)
+        pl.when(sends_edge[e])(whole.wait_send)
 
 
 def finish_kernel(table, ancestors, y, left, mine, right, left_on, right_on, diag, off, out, ext, rows, ext_sem, row_sem):
     u = pl.program_id(0)
     z = lax.rem(lax.axis_index("dev"), 4)
-
-    def pieces(source, first, e):
-        return [
-            pltpu.make_async_copy(
-                source.at[:, pl.ds(4 * q, 4)], ext.at[pl.ds(first, EDGE), pl.ds(4 * q, 4)], ext_sem.at[e, q]
-            )
-            for q in range(4)
-        ]
-
-    middle = pltpu.make_async_copy(mine.at[0], ext.at[pl.ds(EDGE, LOCAL)], ext_sem.at[2, 0])
-    edges = [
-        (pieces(left, 0, 0), pieces(left_on, 0, 0), z == 0),
-        (pieces(right, EDGE + LOCAL, 1), pieces(right_on, EDGE + LOCAL, 1), z == 3),
-    ]
-
-    row_copies = [pltpu.make_async_copy(y.at[v], rows.at[v], row_sem.at[v]) for v in range(LOCAL)]
+    before, after = table[1, 0], table[2, LOCAL - 1] - 1 - table[1, LOCAL - 1]
+
+    def row_copies(v, wait):
+        if wait:
+            pltpu.make_async_copy(y.at[v, pl.ds(0, ANC)], rows.at[v], row_sem.at[v]).wait()
+        else:
+            for a in range(ANC):
+                pltpu.make_async_copy(
+                    y.at[v, ancestors[0, a, table[0, v]]], rows.at[v, a], row_sem.at[v]
+                ).start()
+
+    def tile_copies(t, wait):
+        def copy(source, at, parts):
+            for q in range(0, ANC, ANC // parts):
+                span = pl.ds(q, ANC // parts)
+                ref = source[q // 4 % 2] if isinstance(source, tuple) else source
+                c = pltpu.make_async_copy(ref.at[at, span], ext.at[t, span], ext_sem.at[t])
+                c.wait() if wait else c.start()
+
+        if EDGE <= t < EDGE + LOCAL:
+            copy(mine.at[0], t - EDGE, 1)
+            return
+        if t < EDGE:
+            at, needed, crossed, refs = t, t >= EDGE - before, z == 0, (left, left_on)
+        else:
+            at, refs = t - EDGE - LOCAL, (right, right_on)
+            needed, crossed = at < after, z == 3
+        if wait:
+            pl.when(needed)(lambda: copy(refs[0], at, 1))
+        else:
+            pl.when(needed & crossed)(lambda: copy(refs, at, 4))
+            pl.when(needed & jnp.logical_not(crossed))(lambda: copy(refs[0], at, 1))
 
     @pl.when(u == 0)
     def _():
-        row_copies[0].start()
-        middle.start()
-        for near, far, crossed in edges:
-            for q in range(4):
-                if q % 2:
-                    pl.when(crossed)(far[q].start)
-                    pl.when(jnp.logical_not(crossed))(near[q].start)
-                else:
-                    near[q].start()
-        for c in row_copies[1:]:
-            c.start()
-
-    pltpu.make_async_copy(y.at[u], rows.at[u], row_sem.at[u]).wait()
-    for a in range(ANC):
-        off[0, 0, a * B:(a + 1) * B] = -rows[u, ancestors[0, table[0, u], a]]
+        row_copies(0, False)
+        for t in range(2 * EDGE + LOCAL):
+            tile_copies(t, False)
+        for v in range(1, LOCAL):
+            row_copies(v, False)
+
+    row_copies(u, True)
+    off[0, 0] = -rows[u].reshape(ANC * B, B)
     x = off[0, 0].T
 
     @pl.when(u == 0)
     def _():
-        middle.wait()
-        for near, _, _ in edges:
-            for c in near:
-                c.wait()
+        for t in range(2 * EDGE + LOCAL):
+            tile_copies(t, True)
 
     first = u + EDGE - table[1, u]
     for j in range(0, LOCAL, 2):
@@ -507,13 +525,14 @@
     dma = pltpu.SemaphoreType.DMA
     hbm = pl.BlockSpec(memory_space=pltpu.HBM)
     tiled = panels.reshape(1, LOCAL, ANC, B, B)
+    ancestor_rows = ancestors.swapaxes(1, 2)
     table, spot = pl.pallas_call(
         table_kernel,
         name="table",
         in_specs=[smem, smem],
         out_specs=(smem, smem),
         out_shape=(jax.ShapeDtypeStruct((3, LOCAL), jnp.int32), jax.ShapeDtypeStruct((LOCAL, TILES), jnp.int32)),
-    )(widths, ancestors)
+    )(widths, ancestor_rows)
     y, left, right, left_on, right_on = pl.pallas_call(
         functools.partial(gather_kernel, steps),
         name="gather",
@@ -567,8 +586,8 @@
             out_specs=[unit(ANC * B), unit(LOCAL * B)],
             scratch_shapes=[
                 pltpu.VMEM((2 * EDGE + LOCAL, ANC, B, B), BF16),
-                pltpu.VMEM((LOCAL, TILES, B, B), BF16),
-                dma((3, 4)),
+                pltpu.VMEM((LOCAL, ANC, B, B), BF16),
+                dma((2 * EDGE + LOCAL,)),
                 dma((LOCAL,)),
             ],
         ),
@@ -577,7 +596,7 @@
             jax.ShapeDtypeStruct((1, LOCAL, LOCAL * B, B), BF16),
         ),
         compiler_params=pltpu.CompilerParams(vmem_limit_bytes=62 * 1024 * 1024),
-    )(table, ancestors, y.reshape(LOCAL, TILES, B, B), left, tiled, right, left_on, right_on, diag_inverse)
+    )(table, ancestor_rows, y.reshape(LOCAL, TILES, B, B), left, tiled, right, left_on, right_on, diag_inverse)
     return off, diag
 
 

time: 135 us -> 128 us (0.948); the launches traced: 134 us -> 125 us
  Pallas kernels: 132 us -> 124 us
  local copies, waits for them, and re-layouts: 1.37 us -> 0 us
    pallas_call x1, Pallas kernels: 116 us -> 111 us  [on_device(): pl.pallas_call(functools.partial(gather_kernel, steps), name='gather', ou...]
    pallas_call x1, Pallas kernels: 13.3 us -> 10.9 us  [on_device(): pl.pallas_call(finish_kernel, name='finish', grid_spec=pltpu.PrefetchScal...]
    unnamed x1 -> x0, local copies, waits for them, and re-layouts: 1.37 us -> none
where the time goes in v3:
time: 128 us; the launch traced here: 125 us
  Pallas kernels  124 us (97%)
    pallas_call x1, Pallas kernels, on_device(): pl.pallas_call(functools.partial(gather_kernel, steps), name='gather', ou...  111 us
    pallas_call x1, Pallas kernels, on_device(): pl.pallas_call(finish_kernel, name='finish', grid_spec=pltpu.PrefetchScal...  10.9 us

profile of v3, /device:TPU:1, one launch (start us, length us, event | category | flops | bytes accessed | tf_op | source)
XLA Modules:
  0.0 125.2 jit_solution(9404665939151050706)
XLA Ops:
  0.6 2.5 %table.1 = (s32[3,6]{1,0:T(4,128)}, s32[6,32]{1,0:T(8,128)}) custom-call(s32[1,32]{1,0:T(1,128)} %widths.1, s32[1,16,32]{2,1,0:T(8,128)} %bitcast.6), custom_call_target="tpu_custom_call" | custom-call | tf_op jit(solution)/shard_map/table/pallas_call | solution.py:529
  3.1 111.1 %gather.1 = (bf16[6,8,4,128,128]{4,3,2,1,0:T(8,128)(2,1)}, bf16[5,16,128,128]{3,2,1,0:T(8,128)(2,1)}, bf16[5,16,128,128]{3,2,1,0:T(8,128)(2,1)}, bf16[5,16,128,1...) custom-call(bf16[512,256]{1,0:T(8,128)(2,1)} %sep.1, bf16[1,6,16,128,128]{4,3,2,1,0:T(8,128)(2,1)} %bitcast.3, ...), custom_call_target="tpu_custom_call" | custom-call | tf_op jit(solution)/shard_map/gather/pallas_call | solution.py:536
  114.2 10.9 %finish.1 = (bf16[1,6,2048,128]{3,2,1,0:T(8,128)(2,1)}, bf16[1,6,768,128]{3,2,1,0:T(8,128)(2,1)}) custom-call(s32[3,6]{1,0:T(4,128)} %get-tuple-element.9.table, s32[1,16,32]{2,1,0:T(8,128)} %bitcast.7, bf16[6,32,128,128]{3,2,1,0:T(8,128)(2,1)} %bitcast.5, bf16[5,16,128,128]{3,2,1,0:T(8,128)(2,1)} %get-tuple-element.12.left, ...), custom_call_target="tpu_custom_call" | custom-call | tf_op jit(solution)/shard_map/finish/pallas_call | solution.py:577

commit v4 on v3

--- a/solution.py
+++ b/solution.py
@@ -29,6 +29,7 @@
 KC = 256
 SPREADS = 8
 HALOS = 20
+EDGES = (1, 3, 0, 5, 2, 7, 4, 9, 6, 11, 8, 13, 10, 15, 12, 17, 14, 19, 16, 18)
 
 
 def plan():
@@ -54,7 +55,7 @@
                 heapq.heappush(heap, (free[link] + latency, count("event"), m))
                 steps.append(("send", m))
         while count("pump") and got["edges"] < HALOS and not queue["z", 1] and free["z", 1] < clock + depth:
-            i = got["edges"]
+            i = EDGES[got["edges"]]
             got["edges"] += 1
             for s in (1, -1):
                 free["z", s] = max(clock, free["z", s]) + edge / rate

time: 128 us -> 125 us (0.977); the launches traced: 125 us -> 125 us
  no operation moved by 1% of the time
where the time goes in v4:
time: 125 us
  Pallas kernels  124 us (99%)
    pallas_call x1, Pallas kernels, on_device(): pl.pallas_call(functools.partial(gather_kernel, steps), name='gather', ou...  110 us
    pallas_call x1, Pallas kernels, on_device(): pl.pallas_call(finish_kernel, name='finish', grid_spec=pltpu.PrefetchScal...  11.7 us

profile of v4, /device:TPU:1, one launch (start us, length us, event | category | flops | bytes accessed | tf_op | source)
XLA Modules:
  0.0 125.0 jit_solution(2063342971646026499)
XLA Ops:
  0.6 2.5 %table.1 = (s32[3,6]{1,0:T(4,128)}, s32[6,32]{1,0:T(8,128)}) custom-call(s32[1,32]{1,0:T(1,128)} %widths.1, s32[1,16,32]{2,1,0:T(8,128)} %bitcast.6), custom_call_target="tpu_custom_call" | custom-call | tf_op jit(solution)/shard_map/table/pallas_call | solution.py:530
  3.1 109.9 %gather.1 = (bf16[6,8,4,128,128]{4,3,2,1,0:T(8,128)(2,1)}, bf16[5,16,128,128]{3,2,1,0:T(8,128)(2,1)}, bf16[5,16,128,128]{3,2,1,0:T(8,128)(2,1)}, bf16[5,16,128,1...) custom-call(bf16[512,256]{1,0:T(8,128)(2,1)} %sep.1, bf16[1,6,16,128,128]{4,3,2,1,0:T(8,128)(2,1)} %bitcast.3, ...), custom_call_target="tpu_custom_call" | custom-call | tf_op jit(solution)/shard_map/gather/pallas_call | solution.py:537
  113.1 11.7 %finish.1 = (bf16[1,6,2048,128]{3,2,1,0:T(8,128)(2,1)}, bf16[1,6,768,128]{3,2,1,0:T(8,128)(2,1)}) custom-call(s32[3,6]{1,0:T(4,128)} %get-tuple-element.9.table, s32[1,16,32]{2,1,0:T(8,128)} %bitcast.7, bf16[6,32,128,128]{3,2,1,0:T(8,128)(2,1)} %bitcast.5, bf16[5,16,128,128]{3,2,1,0:T(8,128)(2,1)} %get-tuple-element.12.left, ...), custom_call_target="tpu_custom_call" | custom-call | tf_op jit(solution)/shard_map/finish/pallas_call | solution.py:578

commit v5 on v4

--- a/solution.py
+++ b/solution.py
@@ -61,7 +61,7 @@
                 free["z", s] = max(clock, free["z", s]) + edge / rate
             steps.append(("edge", i))
             if i % 2:
-                heapq.heappush(heap, (free["z", 1] + 2 * latency, count("event"), ("edge", i)))
+                heapq.heappush(heap, (free["z", 1] + 3 * latency, count("event"), ("edge", i)))
 
     def near(part, phase, a):
         for s in (1, -1):

time: 125 us -> 125 us (level); the launches traced: 125 us -> 123 us
  no operation moved by 1% of the time
where the time goes in v5:
time: 125 us; the launch traced here: 123 us
  Pallas kernels  123 us (98%)
    pallas_call x1, Pallas kernels, on_device(): pl.pallas_call(functools.partial(gather_kernel, steps), name='gather', ou...  109 us
    pallas_call x1, Pallas kernels, on_device(): pl.pallas_call(finish_kernel, name='finish', grid_spec=pltpu.PrefetchScal...  11.1 us

profile of v5, /device:TPU:1, one launch (start us, length us, event | category | flops | bytes accessed | tf_op | source)
XLA Modules:
  0.0 123.4 jit_solution(16311204257170488005)
XLA Ops:
  0.6 2.5 %table.1 = (s32[3,6]{1,0:T(4,128)}, s32[6,32]{1,0:T(8,128)}) custom-call(s32[1,32]{1,0:T(1,128)} %widths.1, s32[1,16,32]{2,1,0:T(8,128)} %bitcast.6), custom_call_target="tpu_custom_call" | custom-call | tf_op jit(solution)/shard_map/table/pallas_call | solution.py:530
  3.1 109.0 %gather.1 = (bf16[6,8,4,128,128]{4,3,2,1,0:T(8,128)(2,1)}, bf16[5,16,128,128]{3,2,1,0:T(8,128)(2,1)}, bf16[5,16,128,128]{3,2,1,0:T(8,128)(2,1)}, bf16[5,16,128,1...) custom-call(bf16[512,256]{1,0:T(8,128)(2,1)} %sep.1, bf16[1,6,16,128,128]{4,3,2,1,0:T(8,128)(2,1)} %bitcast.3, ...), custom_call_target="tpu_custom_call" | custom-call | tf_op jit(solution)/shard_map/gather/pallas_call | solution.py:537
  112.1 11.1 %finish.1 = (bf16[1,6,2048,128]{3,2,1,0:T(8,128)(2,1)}, bf16[1,6,768,128]{3,2,1,0:T(8,128)(2,1)}) custom-call(s32[3,6]{1,0:T(4,128)} %get-tuple-element.9.table, s32[1,16,32]{2,1,0:T(8,128)} %bitcast.7, bf16[6,32,128,128]{3,2,1,0:T(8,128)(2,1)} %bitcast.5, bf16[5,16,128,128]{3,2,1,0:T(8,128)(2,1)} %get-tuple-element.12.left, ...), custom_call_target="tpu_custom_call" | custom-call | tf_op jit(solution)/shard_map/finish/pallas_call | solution.py:578
